TPU v7x, 32 devices: a whole 2x2x4 slice. The times are simulated.
32 devices in a mesh: groups: 2 (over y), expert: 4 (over x, core), etp: 4 (over z).
Axes of the slice: x: 2, y: 2, z: 4, core: 2. Of those that a mesh axis runs over, the one named last changes fastest.
Arguments:
- tokens: bfloat16 [1024, 4096], P(('groups', 'expert'), 'etp'), parts along dimension 0, may hold values from -6 to 6
- route_ids: int32 [1024, 2], P(('groups', 'expert')), parts along dimension 0, may hold values from 0 to 3, all different within a row; in each aligned block of 128 rows (0 to 127, 128 to 255, ...) at most 96 rows name the same one
- gate_weights: float32 [1024, 2], P(('groups', 'expert')), parts along dimension 0, may hold values from 0.2 to 1
- w_gate: bfloat16 [4, 4096, 14336], P('expert', None, 'etp'), may hold values from -0.09375 to 0.09375
- w_up: bfloat16 [4, 4096, 14336], P('expert', None, 'etp'), may hold values from -0.09375 to 0.09375
- w_down: bfloat16 [4, 14336, 4096], P('expert', 'etp'), may hold values from -0.0625 to 0.0625
Outputs:
- mixed: bfloat16 [1024, 4096], P(('groups', 'expert'), 'etp'), parts along dimension 0
There are 2 independent parts, one for each index of `groups`. A program takes and returns all parts, laid end to end along the dimension named above; an argument that names none is the same for every part. Nothing has to cross between parts.
Inputs may be any that keep to these rules, and one draw needn't show every extreme that they name: `route_ids`: each row names two different experts. In the rows of one index of expert (128 aligned rows), no expert is named by more than 96 rows, a bound that some block reaches.
All inputs are finite; a program needn't handle non-finite values.
Results may differ from a plain program's by a relative error of at most 0.024.
Values may be sent and summed in bfloat16 or wider, within the bound.
A program may use at most 192 MiB of HBM per device.

v0:
```python
import jax
import jax.numpy as jnp
from jax import lax
from jax.sharding import PartitionSpec as P

CAP = 96


def shards(tokens, route_ids, gate_weights, w_gate, w_up, w_down):
    cycle_size = lax.axis_size("expert")
    token_count, local_width = tokens.shape
    slot_total = cycle_size * CAP
    expert_iota = lax.broadcasted_iota(jnp.int32, (1, 1, cycle_size), 2)
    hit_mask = route_ids[:, :, None] == expert_iota
    routed = jnp.any(hit_mask, axis=1).astype(jnp.int32)
    weighting = jnp.sum(jnp.where(hit_mask, gate_weights[:, :, None], 0.0), axis=1)
    slot_index = jnp.cumsum(routed, axis=0) - 1
    expert_base = lax.broadcasted_iota(jnp.int32, (1, cycle_size), 1) * CAP
    target_slot = jnp.where(routed == 1, expert_base + slot_index, -1)
    slot_iota = lax.broadcasted_iota(jnp.int32, (1, 1, slot_total), 2)
    pick_table = target_slot[:, :, None] == slot_iota
    select_table = jnp.any(pick_table, axis=1).astype(jnp.bfloat16)
    combine_table = jnp.sum(jnp.where(pick_table, weighting[:, :, None], 0.0), axis=1)
    dispatched = jnp.dot(select_table.T, tokens, preferred_element_type=jnp.float32)
    dispatched = dispatched.astype(jnp.bfloat16).reshape(cycle_size, CAP, local_width)
    gate_local = w_gate[0]
    up_local = w_up[0]
    down_local = w_down[0]
    received = lax.all_to_all(dispatched, "expert", split_axis=0, concat_axis=0, tiled=True)
    columns_in = lax.all_gather(
        received.reshape(slot_total, local_width), "etp", axis=1, tiled=True
    )
    gate_sum = jnp.dot(columns_in, gate_local, preferred_element_type=jnp.float32)
    up_sum = jnp.dot(columns_in, up_local, preferred_element_type=jnp.float32)
    hidden = (jax.nn.silu(gate_sum) * up_sum).astype(jnp.bfloat16)
    partial_out = jnp.dot(hidden, down_local, preferred_element_type=jnp.float32).astype(
        jnp.bfloat16
    )
    finished = (
        lax.psum_scatter(partial_out, "etp", scatter_dimension=1, tiled=True)
        .astype(jnp.float32)
        .astype(jnp.bfloat16)
    )
    results = lax.all_to_all(
        finished.reshape(cycle_size, CAP, local_width),
        "expert",
        split_axis=0,
        concat_axis=0,
        tiled=True,
    )
    flat_results = results.reshape(slot_total, local_width).astype(jnp.float32)
    mixed = jnp.dot(combine_table, flat_results, precision=lax.Precision.HIGHEST)
    return mixed.astype(jnp.bfloat16)


def solution(mesh):
    return jax.shard_map(
        shards,
        mesh=mesh,
        in_specs=(
            P(("groups", "expert"), "etp"),
            P(("groups", "expert"), None),
            P(("groups", "expert"), None),
            P("expert", None, "etp"),
            P("expert", None, "etp"),
            P("expert", "etp", None),
        ),
        out_specs=P(("groups", "expert"), "etp"),
        check_vma=False,
    )
```

profile of v0, /device:TPU:0, one launch (start us, length us, event | category | flops | bytes accessed | tf_op | source)
XLA Modules:
  0.0 231.4 jit_solution(1056805115542354805)
XLA Ops:
  6.5 0.0 all-gather.2.cloned.1.call-start
  6.5 0.7 fusion.18
  7.3 0.1 copy.14
  7.4 0.2 reduce_window_sum.11
  7.6 0.1 copy.15
  7.6 0.1 add_select_fusion
  7.7 0.2 fusion.17
  7.9 0.4 convolution_convert_fusion
  8.3 15.8 %all_to_all.10 = bf16[4,96,1024]{2,1,0:T(8,128)(2,1)} all-to-all(bf16[4,96,1024]{2,1,0:T(8,128)(2,1)S(1)} %bitcast.37), channel_id=1, replica_groups=mesh['groups'=2,'expert'=4,'etp'=4] {'expert'}, dimensions={0} | all-to-all | bytes 1572864 | tf_op jit(solution)/shard_map/all_to_all | solution.py:29
  24.1 0.0 all-gather.2.cloned.1.call-update
  24.1 0.0 reduce-scatter.2.cloned.1.call-start
  24.2 64.3 %all-gather.2.cloned.1.call-done = bf16[384,4096]{1,0:T(8,128)(2,1)} async-done(((bf16[384,1024]{1,0:T(8,128)(2,1)}), bf16[384,4096]{1,0:T(8,128)(2,1)}) %all-gather.2.cloned.1.call-update) | async-done | bytes 3145744 | tf_op jit(solution)/shard_map/all_gather | solution.py:30
  88.5 23.5 %fusion.4 = f32[384,3584]{1,0:T(8,128)} fusion(bf16[384,4096]{1,0:T(8,128)(2,1)} %all-gather.2.cloned.1.call-done, bf16[1,4096,3584]{2,1,0:T(8,128)(2,1)} %param.9), kind=kOutput, calls=%fused_computation.4 | convolution fusion | flops 11274289152 | bytes 38010880 | tf_op jit(solution)/shard_map/dot_general | solution.py:33
  112.0 18.2 %fusion.12.clone.4 = bf16[384,3584]{1,0:T(8,128)(2,1)S(1)} fusion(bf16[384,4096]{1,0:T(8,128)(2,1)S(1)} %copy-done.4, bf16[1,4096,3584]{2,1,0:T(8,128)(2,1)} %param.10, f32[384,3584]{1,0:T(8,128)} %fusion.4), kind=kOutput, calls=%fused_computation.8.clone.clone.clone.1 | convolution fusion | flops 11282546688 | bytes 40763392 | tf_op jit(solution)/shard_map/dot_general | solution.py:34
  130.2 0.0 copy-start.2
  130.2 0.0 copy-start.3
  130.2 0.0 copy-start.1
  130.2 18.7 %fusion.9 = bf16[384,4096]{1,0:T(8,128)(2,1)} fusion(bf16[1,3584,4096]{2,1,0:T(8,128)(2,1)} %param.11, bf16[384,3584]{1,0:T(8,128)(2,1)S(1)} %fusion.12.clone.4), kind=kOutput, calls=%fused_computation.7 | convolution fusion | flops 11275862016 | bytes 35258368 | tf_op jit(solution)/shard_map/dot_general | solution.py:36
  149.0 0.0 reduce-scatter.2.cloned.1.call-update
  149.0 59.2 %reduce-scatter.2.cloned.1.call-done = bf16[384,1024]{1,0:T(8,128)(2,1)} async-done(((bf16[384,4096]{1,0:T(8,128)(2,1)}), bf16[384,1024]{1,0:T(8,128)(2,1)}) %reduce-scatter.2.cloned.1.call-update) | async-done | bytes 786448 | tf_op jit(solution)/shard_map/reduce_scatter | solution.py:40
  208.2 3.5 %all-to-all-start.1 = ((bf16[4,96,1024]{2,1,0:T(8,128)(2,1)}), bf16[4,96,1024]{2,1,0:T(8,128)(2,1)S(1)}, u32[]{:S(2)}, u32[]{:S(2)}) async-start(bf16[4,96,1024]{2,1,0:T(8,128)(2,1)} %bitcast.38), calls=%async_computation.2 | async-start | bytes 1572864 | tf_op jit(solution)/shard_map/all_to_all | solution.py:44
  211.7 0.2 select_reduce_fusion
  211.9 11.3 %all-to-all-done.1 = bf16[4,96,1024]{2,1,0:T(8,128)(2,1)S(1)} async-done(((bf16[4,96,1024]{2,1,0:T(8,128)(2,1)}), bf16[4,96,1024]{2,1,0:T(8,128)(2,1)S(1)}, u32[]{:S(2)}, u32[]{:S(2)}) %all-to-all-start.1) | async-done | bytes 786464 | tf_op jit(solution)/shard_map/all_to_all | solution.py:44
  223.3 1.3 convolution_convert_fusion.1
  (10 shorter events, 0.0 us)
Async XLA Ops:
  6.5 1.4 copy-start
  6.5 81.9 %all-gather.2.cloned.1.call-start = ((), (), s32[]{:S(2)}) async-start(), calls=%async_computation.3 | async-start | bytes 3932160 | tf_op jit(solution)/shard_map/all_gather | solution.py:30
  24.1 184.1 %reduce-scatter.2.cloned.1.call-start = ((), (), s32[]{:S(2)}) async-start(), calls=%async_computation.4 | async-start | bytes 3932160 | tf_op jit(solution)/shard_map/reduce_scatter | solution.py:40
  88.5 23.5 %copy-start.4 = (bf16[384,4096]{1,0:T(8,128)(2,1)S(1)}, bf16[384,4096]{1,0:T(8,128)(2,1)}, u32[]{:S(2)}) copy-start(bf16[384,4096]{1,0:T(8,128)(2,1)} %all-gather.2.cloned.1.call-done) | copy-start | bytes 9437188
  130.2 81.5 %copy-start.2 = (f32[128,2]{0,1:T(2,128)S(1)}, f32[128,2]{0,1:T(2,128)}, u32[]{:S(2)}) copy-start(f32[128,2]{0,1:T(2,128)} %param.8) | copy-start | bytes 3076
  130.2 81.5 %copy-start.3 = (s32[128,2]{0,1:T(2,128)S(1)}, s32[128,2]{0,1:T(2,128)}, u32[]{:S(2)}) copy-start(s32[128,2]{0,1:T(2,128)} %param.7) | copy-start | bytes 3076
  130.2 94.3 %copy-start.1 = (bf16[128,1024]{1,0:T(8,128)(2,1)S(1)}, bf16[128,1024]{1,0:T(8,128)(2,1)}, u32[]{:S(2)}) copy-start(bf16[128,1024]{1,0:T(8,128)(2,1)} %param.6) | copy-start | bytes 786436
  208.2 15.1 %all-to-all-start.1 = ((bf16[4,96,1024]{2,1,0:T(8,128)(2,1)}), bf16[4,96,1024]{2,1,0:T(8,128)(2,1)S(1)}, u32[]{:S(2)}, u32[]{:S(2)}) async-start(bf16[4,96,1024]{2,1,0:T(8,128)(2,1)} %bitcast.38), calls=%async_computation.2 | async-start | bytes 1572864 | tf_op jit(solution)/shard_map/all_to_all | solution.py:44
Sparse Core Ops, SparseCore 0:
  24.2 64.1 all-gather.1
  149.1 59.0 reduce-scatter.1
where the time goes:
time: 232 us; the launch traced here: 231 us
  waiting for transfers between devices  135 us (58%)
  matrix products  62.1 us (27%)
  blocking collectives  15.8 us (7%)
  between operations  13.5 us (6%)
  starting transfers between devices  3.54 us (2%)
    all_gather x1, waiting for transfers between devices, shards(): lax.all_gather(received.reshape(slot_total, local_width), 'etp', axis=1,...  64.3 us
    reduce_scatter x1, waiting for transfers between devices, shards(): lax.psum_scatter(partial_out, 'etp', scatter_dimension=1, tiled=True)  59.2 us
    dot_general x1, matrix products, shards(): jnp.dot(columns_in, gate_local, preferred_element_type=jnp.float32)  23.5 us
    dot_general x1, matrix products, shards(): jnp.dot(hidden, down_local, preferred_element_type=jnp.float32)  18.7 us
    dot_general x1, matrix products, shards(): up_sum = jnp.dot(columns_in, up_local, preferred_element_type=jnp.float32)  18.2 us
    all_to_all x1, blocking collectives, shards(): lax.all_to_all(dispatched, 'expert', split_axis=0, concat_axis=0, tiled=T...  15.8 us
    all_to_all x1, waiting for transfers between devices, shards(): lax.all_to_all(finished.reshape(cycle_size, CAP, local_width), 'expert',...  11.3 us
  transfers between devices with their start and end apart: 3, of which 3 were waited for; matrix products, arithmetic and copies ran while one was open for 0% of the time, Pallas kernels for 0%

commit v1 on v0

--- a/solution.py
+++ b/solution.py
@@ -27,9 +27,9 @@
     up_local = w_up[0]
     down_local = w_down[0]
     received = lax.all_to_all(dispatched, "expert", split_axis=0, concat_axis=0, tiled=True)
-    columns_in = lax.all_gather(
-        received.reshape(slot_total, local_width), "etp", axis=1, tiled=True
-    )
+    part = received.reshape(slot_total, local_width)
+    shards_2 = lax.all_gather(part, "etp", axis=0, tiled=False)
+    columns_in = jnp.concatenate(shards_2, axis=1)
     gate_sum = jnp.dot(columns_in, gate_local, preferred_element_type=jnp.float32)
     up_sum = jnp.dot(columns_in, up_local, preferred_element_type=jnp.float32)
     hidden = (jax.nn.silu(gate_sum) * up_sum).astype(jnp.bfloat16)

time: 232 us -> 230 us (level)
  matrix products: 62.1 us -> 57.3 us
  local copies, waits for them, and re-layouts: 0.2 us -> 3.62 us
    dot_general x1, matrix products: 23.5 us -> 17.8 us  [shards(): jnp.dot(columns_in, gate_local, preferred_element_type=jnp.float32)]
    all_gather x0 -> x1, local copies, waits for them, and re-layouts: none -> 3.42 us  [shards(): shards_2 = lax.all_gather(part, 'etp', axis=0, tiled=False)]
where the time goes in v1:
time: 230 us
  waiting for transfers between devices  135 us (59%)
  matrix products  57.3 us (25%)
  blocking collectives  15.8 us (7%)
  between operations  13.5 us (6%)
  local copies, waits for them, and re-layouts  3.62 us (2%)
  starting transfers between devices  3.54 us (2%)
    all_gather x1, waiting for transfers between devices, shards(): shards_2 = lax.all_gather(part, 'etp', axis=0, tiled=False)  64.3 us
    reduce_scatter x1, waiting for transfers between devices, shards(): lax.psum_scatter(partial_out, 'etp', scatter_dimension=1, tiled=True)  59.2 us
    dot_general x1, matrix products, shards(): up_sum = jnp.dot(columns_in, up_local, preferred_element_type=jnp.float32)  19 us
    dot_general x1, matrix products, shards(): jnp.dot(hidden, down_local, preferred_element_type=jnp.float32)  18.7 us
    dot_general x1, matrix products, shards(): jnp.dot(columns_in, gate_local, preferred_element_type=jnp.float32)  17.8 us
    all_to_all x1, blocking collectives, shards(): lax.all_to_all(dispatched, 'expert', split_axis=0, concat_axis=0, tiled=T...  15.8 us
    all_to_all x1, waiting for transfers between devices, shards(): lax.all_to_all(finished.reshape(cycle_size, CAP, local_width), 'expert',...  11.3 us
  transfers between devices with their start and end apart: 3, of which 3 were waited for; matrix products, arithmetic and copies ran while one was open for 0% of the time, Pallas kernels for 0%

profile of v1, /device:TPU:0, one launch (start us, length us, event | category | flops | bytes accessed | tf_op | source)
XLA Modules:
  0.0 230.0 jit_solution(14004975144004933193)
XLA Ops:
  6.5 0.7 fusion.18
  7.3 0.1 copy.24
  7.4 0.2 reduce_window_sum.11
  7.6 0.1 copy.25
  7.6 0.1 add_select_fusion
  7.7 0.2 fusion.17
  7.9 0.4 convolution_convert_fusion
  8.3 15.8 %all_to_all.10 = bf16[4,96,1024]{2,1,0:T(8,128)(2,1)} all-to-all(bf16[4,96,1024]{2,1,0:T(8,128)(2,1)S(1)} %bitcast.42), channel_id=1, replica_groups=mesh['groups'=2,'expert'=4,'etp'=4] {'expert'}, dimensions={0} | all-to-all | bytes 1572864 | tf_op jit(solution)/shard_map/all_to_all | solution.py:29
  24.1 0.0 all-gather.2.cloned.1.call-update
  24.1 0.0 reduce-scatter.2.cloned.1.call-start
  24.2 64.3 %all-gather.2.cloned.1.call-done = bf16[4,384,1024]{2,1,0:T(8,128)(2,1)} async-done(((bf16[1,384,1024]{2,1,0:T(8,128)(2,1)}), bf16[4,384,1024]{2,1,0:T(8,128)(2,1)}) %all-gather.2.cloned.1.call-update) | async-done | bytes 3145744 | tf_op jit(solution)/shard_map/all_gather | solution.py:31
  88.5 3.4 %copy.26 = bf16[4,384,1024]{1,2,0:T(8,128)(2,1)S(1)} copy(bf16[4,384,1024]{2,1,0:T(8,128)(2,1)} %all-gather.2.cloned.1.call-done) | data formatting | bytes 6291456 | tf_op jit(solution)/shard_map/all_gather | solution.py:31
  91.9 17.8 %fusion.4 = f32[384,3584]{1,0:T(8,128)} fusion(bf16[384,4096]{0,1:T(8,128)(2,1)S(1)} %bitcast.38, bf16[1,4096,3584]{2,1,0:T(8,128)(2,1)} %param.9), kind=kOutput, calls=%fused_computation.4 | convolution fusion | flops 11274289152 | bytes 38010880 | tf_op jit(solution)/shard_map/dot_general | solution.py:33
  109.8 19.0 %fusion.12.clone.4 = bf16[384,3584]{1,0:T(8,128)(2,1)S(1)} fusion(bf16[384,4096]{0,1:T(8,128)(2,1)S(1)} %bitcast.39, bf16[1,4096,3584]{2,1,0:T(8,128)(2,1)} %param.10, f32[384,3584]{1,0:T(8,128)} %fusion.4), kind=kOutput, calls=%fused_computation.8.clone.clone.clone.1 | convolution fusion | flops 11282546688 | bytes 40763392 | tf_op jit(solution)/shard_map/dot_general | solution.py:34
  128.8 0.0 copy-start.2
  128.8 0.0 copy-start.3
  128.8 0.0 copy-start.1
  128.8 18.7 %fusion.9 = bf16[384,4096]{1,0:T(8,128)(2,1)} fusion(bf16[1,3584,4096]{2,1,0:T(8,128)(2,1)} %param.11, bf16[384,3584]{1,0:T(8,128)(2,1)S(1)} %fusion.12.clone.4), kind=kOutput, calls=%fused_computation.7 | convolution fusion | flops 11275862016 | bytes 35258368 | tf_op jit(solution)/shard_map/dot_general | solution.py:36
  147.5 0.0 reduce-scatter.2.cloned.1.call-update
  147.5 59.2 %reduce-scatter.2.cloned.1.call-done = bf16[384,1024]{1,0:T(8,128)(2,1)} async-done(((bf16[384,4096]{1,0:T(8,128)(2,1)}), bf16[384,1024]{1,0:T(8,128)(2,1)}) %reduce-scatter.2.cloned.1.call-update) | async-done | bytes 786448 | tf_op jit(solution)/shard_map/reduce_scatter | solution.py:40
  206.8 3.5 %all-to-all-start.1 = ((bf16[4,96,1024]{2,1,0:T(8,128)(2,1)}), bf16[4,96,1024]{2,1,0:T(8,128)(2,1)S(1)}, u32[]{:S(2)}, u32[]{:S(2)}) async-start(bf16[4,96,1024]{2,1,0:T(8,128)(2,1)} %bitcast.43), calls=%async_computation.2 | async-start | bytes 1572864 | tf_op jit(solution)/shard_map/all_to_all | solution.py:44
  210.3 0.2 select_reduce_fusion
  210.5 11.3 %all-to-all-done.1 = bf16[4,96,1024]{2,1,0:T(8,128)(2,1)S(1)} async-done(((bf16[4,96,1024]{2,1,0:T(8,128)(2,1)}), bf16[4,96,1024]{2,1,0:T(8,128)(2,1)S(1)}, u32[]{:S(2)}, u32[]{:S(2)}) %all-to-all-start.1) | async-done | bytes 786464 | tf_op jit(solution)/shard_map/all_to_all | solution.py:44
  221.8 1.3 convolution_convert_fusion.1
  (9 shorter events, 0.0 us)
Async XLA Ops:
  6.5 1.4 copy-start
  6.5 82.0 %all-gather.2.cloned.1.call-start = ((), (), s32[]{:S(2)}) async-start(), calls=%async_computation.3 | async-start | bytes 3932160 | tf_op jit(solution)/shard_map/all_gather | solution.py:31
  24.1 182.6 %reduce-scatter.2.cloned.1.call-start = ((), (), s32[]{:S(2)}) async-start(), calls=%async_computation.4 | async-start | bytes 3932160 | tf_op jit(solution)/shard_map/reduce_scatter | solution.py:40
  128.8 81.5 %copy-start.2 = (f32[128,2]{0,1:T(2,128)S(1)}, f32[128,2]{0,1:T(2,128)}, u32[]{:S(2)}) copy-start(f32[128,2]{0,1:T(2,128)} %param.8) | copy-start | bytes 3076
  128.8 81.5 %copy-start.3 = (s32[128,2]{0,1:T(2,128)S(1)}, s32[128,2]{0,1:T(2,128)}, u32[]{:S(2)}) copy-start(s32[128,2]{0,1:T(2,128)} %param.7) | copy-start | bytes 3076
  128.8 94.3 %copy-start.1 = (bf16[128,1024]{1,0:T(8,128)(2,1)S(1)}, bf16[128,1024]{1,0:T(8,128)(2,1)}, u32[]{:S(2)}) copy-start(bf16[128,1024]{1,0:T(8,128)(2,1)} %param.6) | copy-start | bytes 786436
  206.8 15.1 %all-to-all-start.1 = ((bf16[4,96,1024]{2,1,0:T(8,128)(2,1)}), bf16[4,96,1024]{2,1,0:T(8,128)(2,1)S(1)}, u32[]{:S(2)}, u32[]{:S(2)}) async-start(bf16[4,96,1024]{2,1,0:T(8,128)(2,1)} %bitcast.43), calls=%async_computation.2 | async-start | bytes 1572864 | tf_op jit(solution)/shard_map/all_to_all | solution.py:44
Sparse Core Ops, SparseCore 0:
  24.2 64.2 all-gather.1
  147.7 59.0 reduce-scatter.1
